TPU v7x, 32 devices: a whole 2x2x4 slice. The times are simulated.
32 devices in a mesh: lat: 4 (over z), lon: 8 (over y, x, core).
Axes of the slice: x: 2, y: 2, z: 4, core: 2. Of those that a mesh axis runs over, the one named last changes fastest.
Arguments:
- increments: bfloat16 [65536, 3, 128], P(('lat', 'lon')), may hold values from -6 to 6
- cotangent: bfloat16 [65536, 128], P(('lat', 'lon')), may hold values from -6 to 6
- owner_perm: int32 [32, 2048], P(('lat', 'lon')), may hold values from 0 to 2047, each once within a row
- coarse_index: int32 [2, 32768], P(None, ('lat', 'lon')), may hold values from 0 to 2047
- coarse_weight: float32 [32768], P(('lat', 'lon')), may hold values from 0.2 to 0.8
- back_index: int32 [2, 65536], P(None, ('lat', 'lon')), may hold values from 0 to 1023
- back_weight: float32 [65536], P(('lat', 'lon')), may hold values from 0.2 to 0.8
- lw_scale: float32 [16, 32768], P(None, ('lat', 'lon')), may hold values from 0.1 to 1
- sw_scale: float32 [14, 32768], P(None, ('lat', 'lon')), may hold values from 0.2 to 2
- sunlit: int32 [32768], P(('lat', 'lon')), may hold values from 0 to 1, as said below
- lw_table: bfloat16 [16, 3, 128, 128], P(None, None, 'lon'), may hold values from -0.3125 to 0.3125
- sw_table: bfloat16 [14, 3, 128, 128], P(None, None, 'lon'), may hold values from -0.3125 to 0.3125
Outputs:
- tendency: bfloat16 [65536, 128], P(('lat', 'lon'))
- gradient: bfloat16 [65536, 3, 128], P(('lat', 'lon'))
Inputs may be any that keep to these rules, and one draw needn't show every extreme that they name: In each device's block of 1024 radiation columns at most 640 are sunlit, and some device has exactly 640.
All inputs are finite; a program needn't handle non-finite values.
Results may differ from a plain program's by a relative error of at most 0.014.
Values may be sent and summed in bfloat16 or wider, within the bound.
A program may use at most 64 MiB of HBM per device.

v0:
```python
import jax
import jax.numpy as jnp
from jax import lax
from jax.sharding import PartitionSpec as P


def block_split(row_count):
    block = 512
    return (block, row_count // block)


def band_sum(coarse, band_table, band_scale):
    row_count = coarse.shape[0]
    block, blocks = block_split(row_count)
    coarse_blocks = coarse.reshape(blocks, block, coarse.shape[1])
    scale_blocks = band_scale.reshape(band_scale.shape[0], blocks, block).swapaxes(0, 1)

    def one_block(pair):
        product = jnp.einsum("rc,bck->rbk", pair[0], band_table, preferred_element_type=jnp.float32)
        return jnp.einsum("br,rbk->rk", pair[1], product)

    return lax.map(one_block, (coarse_blocks, scale_blocks)).reshape(row_count, band_table.shape[2])


def band_adjoint(adjoint_coarse, band_table, band_scale):
    row_count = adjoint_coarse.shape[0]
    block, blocks = block_split(row_count)
    adjoint_blocks = adjoint_coarse.reshape(blocks, block, adjoint_coarse.shape[1])
    scale_blocks = band_scale.reshape(band_scale.shape[0], blocks, block).swapaxes(0, 1)

    def one_block(pair):
        lifted = (pair[1].T[:, :, None] * pair[0][:, None, :]).astype(jnp.bfloat16)
        return jnp.einsum("rbk,bck->rc", lifted, band_table, preferred_element_type=jnp.float32)

    return lax.map(one_block, (adjoint_blocks, scale_blocks)).reshape(
        row_count, band_table.shape[1]
    )


def spread_back(values, index_pair, weight, target_count):
    source_count = values.shape[0]
    block, blocks = block_split(source_count)
    width = values.shape[1]
    targets = jnp.arange(target_count, dtype=jnp.int32)

    def one_block(total, item):
        rows, first, second, share = item
        table = share[:, None] * (first[:, None] == targets[None, :]).astype(jnp.float32)
        table = table + (1.0 - share)[:, None] * (second[:, None] == targets[None, :]).astype(
            jnp.float32
        )
        added = jnp.einsum(
            "nt,nw->tw",
            table,
            rows,
            precision=lax.Precision.HIGHEST,
            preferred_element_type=jnp.float32,
        )
        return (total + added, None)

    start = jnp.zeros((target_count, width), jnp.float32)
    items = (
        values.reshape(blocks, block, width),
        index_pair[0].reshape(blocks, block),
        index_pair[1].reshape(blocks, block),
        weight.reshape(blocks, block),
    )
    total, unused = lax.scan(one_block, start, items)
    return total


def local(
    increments,
    cotangent,
    owner_perm,
    coarse_index,
    coarse_weight,
    back_index,
    back_weight,
    lw_scale,
    sw_scale,
    sunlit,
    lw_table,
    sw_table,
):
    lw_full, sw_full = (
        lax.all_gather(lw_table, "lon", axis=2, tiled=True),
        lax.all_gather(sw_table, "lon", axis=2, tiled=True),
    )
    level_count = lw_full.shape[3]
    lw_bands = lw_full.reshape(lw_full.shape[0], -1, level_count)
    sw_bands = sw_full.reshape(sw_full.shape[0], -1, level_count)
    order_map = owner_perm[0]
    col_count = increments.shape[0]
    sent_fields = increments[order_map]
    sent_cotangent = cotangent[order_map]
    fields, cot_rad = (
        lax.all_to_all(sent_fields, ("lat", "lon"), split_axis=0, concat_axis=0, tiled=True),
        lax.all_to_all(sent_cotangent, ("lat", "lon"), split_axis=0, concat_axis=0, tiled=True),
    )
    row_count = coarse_weight.shape[0]
    flat_rows = fields.reshape(col_count, -1)
    first = flat_rows[coarse_index[0]].astype(jnp.float32)
    second = flat_rows[coarse_index[1]].astype(jnp.float32)
    coarse = (coarse_weight[:, None] * first + (1.0 - coarse_weight)[:, None] * second).astype(
        jnp.bfloat16
    )
    heating = band_sum(coarse, lw_bands, lw_scale)
    cot_float = cot_rad.astype(jnp.float32)
    adjoint_coarse = spread_back(cot_float, back_index, back_weight, row_count)
    adjoint_rows = band_adjoint(adjoint_coarse, lw_bands, lw_scale)
    sw_weight = sw_scale * sunlit.astype(jnp.float32)[None, :]
    heating = heating + band_sum(coarse, sw_bands, sw_weight)
    adjoint_rows = adjoint_rows + band_adjoint(adjoint_coarse, sw_bands, sw_weight)
    tendency_rad = (
        back_weight[:, None] * heating[back_index[0]]
        + (1.0 - back_weight)[:, None] * heating[back_index[1]]
    ).astype(jnp.bfloat16)
    gradient_rad = spread_back(adjoint_rows, coarse_index, coarse_weight, col_count).astype(
        jnp.bfloat16
    )
    gradient_rad = gradient_rad.reshape(increments.shape)
    back_tendency, back_gradient = (
        lax.all_to_all(tendency_rad, ("lat", "lon"), split_axis=0, concat_axis=0, tiled=True),
        lax.all_to_all(gradient_rad, ("lat", "lon"), split_axis=0, concat_axis=0, tiled=True),
    )
    inverse_map = (
        jnp.zeros((col_count,), jnp.int32).at[order_map].set(jnp.arange(col_count, dtype=jnp.int32))
    )
    tendency = back_tendency[inverse_map]
    gradient = back_gradient[inverse_map]
    return (tendency, gradient)


def solution(mesh):
    in_specs = (
        P(("lat", "lon"), None, None),
        P(("lat", "lon"), None),
        P(("lat", "lon"), None),
        P(None, ("lat", "lon")),
        P(("lat", "lon")),
        P(None, ("lat", "lon")),
        P(("lat", "lon")),
        P(None, ("lat", "lon")),
        P(None, ("lat", "lon")),
        P(("lat", "lon")),
        P(None, None, "lon", None),
        P(None, None, "lon", None),
    )
    out_specs = (P(("lat", "lon"), None), P(("lat", "lon"), None, None))
    return jax.shard_map(local, mesh=mesh, in_specs=in_specs, out_specs=out_specs, check_vma=False)
```

profile of v0, /device:TPU:0, one launch (start us, length us, event | category | flops | bytes accessed | tf_op | source)
XLA Modules:
  0.0 280.1 jit_solution(17873464175656073959)
XLA Ops:
  7.2 0.7 all-gather.5.cloned.1.call-update
  7.9 0.7 compare_select_fusion.2
  8.7 8.8 %gather_fusion.6 = bf16[2048,128]{1,0:T(8,128)(2,1)} fusion(bf16[2048,128]{1,0:T(8,128)(2,1)} %param.25, s32[2048]{0:T(1024)S(1)} %broadcast_clamp_fusion.2), kind=kCustom, calls=%fused_computation.6 | custom fusion | bytes 1056768 | tf_op jit(solution)/shard_map/gather | solution.py:96
  17.5 7.3 %all-to-all-start.2 = ((bf16[32,64,128]{2,1,0:T(8,128)(2,1)}), bf16[32,64,128]{2,1,0:T(8,128)(2,1)S(1)}, u32[]{:S(2)}, u32[]{:S(2)}) async-start(bf16[32,64,128]{2,1,0:T(8,128)(2,1)} %bitcast.45), calls=%async_computation.2 | async-start | bytes 1048576 | tf_op jit(solution)/shard_map/all_to_all | solution.py:99
  24.8 0.0 all-gather.3.cloned.1.call-start
  24.9 0.7 all-gather.3.cloned.1.call-update
  25.6 0.1 mul.118
  25.8 18.4 %gather_fusion = bf16[2048,3,128]{2,0,1:T(8,128)(2,1)} fusion(bf16[2048,3,128]{2,0,1:T(8,128)(2,1)S(1)} %copy-done, s32[2048]{0:T(1024)S(1)} %broadcast_clamp_fusion.2), kind=kCustom, calls=%fused_computation | custom fusion | bytes 3153920 | tf_op jit(solution)/shard_map/gather | solution.py:95
  44.2 4.2 %copy.25 = bf16[2048,3,128]{2,1,0:T(4,128)(2,1)} copy(bf16[2048,3,128]{2,0,1:T(8,128)(2,1)} %gather_fusion) | data formatting | bytes 3145728 | tf_op jit(solution)/shard_map/gather | solution.py:95
  48.5 0.1 reshape.254
  48.6 0.1 reshape.251
  48.7 0.1 mul.129
  48.9 6.1 %all-to-all-start = ((bf16[2048,3,128]{2,1,0:T(4,128)(2,1)}), bf16[2048,3,128]{2,1,0:T(4,128)(2,1)}, u32[]{:S(2)}, u32[]{:S(2)}) async-start(bf16[2048,3,128]{2,1,0:T(4,128)(2,1)} %copy.25), calls=%async_computation | async-start | bytes 4194304 | tf_op jit(solution)/shard_map/all_to_all | solution.py:98
  55.1 1.0 bitcast_convert_fusion
  56.1 19.9 %while.68 = (s32[]{:T(128)}, f32[1024,128]{1,0:T(8,128)S(1)}, s32[4,512]{1,0:T(4,128)S(1)}, f32[4,512]{1,0:T(4,128)S(1)}, s32[4,512]{1,0:T(4,128)S(1)}, /*index=5*/f32[4,512,128]{2,1,0:T(8,128)}, s32[]{:T(128)}, s32[]{:T(128)}) while((s32[]{:T(128)}, f32[1024,128]{1,0:T(8,128)S(1)}, s32[4,512]{1,0:T(4,128)S(1)}, ...), condition=%wide.region_6.7_spmd.clone.clone, body=%wide.region_5.6_spmd.clone.clone.sunk | while | flops 808190464 | bytes 1335911 | solution.py:68
  56.1 4.9 %fusion.109 = f32[1024,128]{1,0:T(8,128)S(1)} fusion(f32[512]{0:T(512)S(1)} %broadcast_subtract_fusion.6, s32[512]{0:T(512)S(1)} %bitcast.170, f32[512]{0:T(512)S(1)} %bitcast.167, s32[512]{0:T(512)S(1)} %bitcast.171, f32[1024,128]{1,0:T(8,128)S(1)} %get-tuple-element.653, f32[4,512,128]{2,1,0:T(8,128)} %get-tuple-element.665, ...), kind=kOutput, calls=%fused_computation.49.clone.1 | convolution fusion | flops 808189952 | bytes 1319425 | tf_op jit(solution)/shard_map/while/body/eval_jaxpr/nt,nw->tw/dot_general | solution.py:52
  61.1 4.9 %fusion.109 = f32[1024,128]{1,0:T(8,128)S(1)} fusion(f32[512]{0:T(512)S(1)} %broadcast_subtract_fusion.6, s32[512]{0:T(512)S(1)} %bitcast.170, f32[512]{0:T(512)S(1)} %bitcast.167, s32[512]{0:T(512)S(1)} %bitcast.171, f32[1024,128]{1,0:T(8,128)S(1)} %get-tuple-element.653, f32[4,512,128]{2,1,0:T(8,128)} %get-tuple-element.665, ...), kind=kOutput, calls=%fused_computation.49.clone.1 | convolution fusion | flops 808189952 | bytes 1319425 | tf_op jit(solution)/shard_map/while/body/eval_jaxpr/nt,nw->tw/dot_general | solution.py:52
  66.1 4.9 %fusion.109 = f32[1024,128]{1,0:T(8,128)S(1)} fusion(f32[512]{0:T(512)S(1)} %broadcast_subtract_fusion.6, s32[512]{0:T(512)S(1)} %bitcast.170, f32[512]{0:T(512)S(1)} %bitcast.167, s32[512]{0:T(512)S(1)} %bitcast.171, f32[1024,128]{1,0:T(8,128)S(1)} %get-tuple-element.653, f32[4,512,128]{2,1,0:T(8,128)} %get-tuple-element.665, ...), kind=kOutput, calls=%fused_computation.49.clone.1 | convolution fusion | flops 808189952 | bytes 1319425 | tf_op jit(solution)/shard_map/while/body/eval_jaxpr/nt,nw->tw/dot_general | solution.py:52
  71.1 4.9 %fusion.109 = f32[1024,128]{1,0:T(8,128)S(1)} fusion(f32[512]{0:T(512)S(1)} %broadcast_subtract_fusion.6, s32[512]{0:T(512)S(1)} %bitcast.170, f32[512]{0:T(512)S(1)} %bitcast.167, s32[512]{0:T(512)S(1)} %bitcast.171, f32[1024,128]{1,0:T(8,128)S(1)} %get-tuple-element.653, f32[4,512,128]{2,1,0:T(8,128)} %get-tuple-element.665, ...), kind=kOutput, calls=%fused_computation.49.clone.1 | convolution fusion | flops 808189952 | bytes 1319425 | tf_op jit(solution)/shard_map/while/body/eval_jaxpr/nt,nw->tw/dot_general | solution.py:52
  76.0 1.2 broadcast.138.clone.1
  77.3 6.9 %while.67 = (s32[]{:T(128)}, f32[2,512,384]{2,1,0:T(8,128)}, f32[2,14,512]{2,1,0:T(8,128)S(1)}, f32[2,512,128]{2,1,0:T(8,128)S(1)}, bf16[14,384,128]{2,1,0:T(8,128)(2,1)}, /*index=5*/s32[]{:T(128)}) while((s32[]{:T(128)}, f32[2,512,384]{2,1,0:T(8,128)}, f32[2,14,512]{2,1,0:T(8,128)S(1)}, f32[2,512,128]{2,1,0:T(8,128)S(1)}, ...), condition=%wide.region_10.11_spmd, body=%wide.region_9.10_spmd.sunk | while | flops 706478080 | bytes 3035725 | solution.py:35
  77.3 3.4 %fusion.106 = f32[2,512,384]{2,1,0:T(8,128)} fusion(f32[2,512,384]{2,1,0:T(8,128)} %get-tuple-element.693, s32[]{:T(128)} %get-tuple-element.692, bf16[14,384,128]{2,1,0:T(8,128)(2,1)} %get-tuple-element.702, f32[512,128]{1,0:T(8,128)S(1)} %dynamic-slice_bitcast_fusion.16, f32[512,14]{0,1:T(8,128)S(1)} %dynamic-slice_bitcast_fusion.17), kind=kOutput, calls=%fused_computation.40.clone.1 | convolution fusion | flops 706478080 | bytes 2454016 | tf_op jit(solution)/shard_map/while/body/eval_jaxpr/rbk,bck->rc/dot_general | solution.py:33
  80.8 3.4 %fusion.106 = f32[2,512,384]{2,1,0:T(8,128)} fusion(f32[2,512,384]{2,1,0:T(8,128)} %get-tuple-element.693, s32[]{:T(128)} %get-tuple-element.692, bf16[14,384,128]{2,1,0:T(8,128)(2,1)} %get-tuple-element.702, f32[512,128]{1,0:T(8,128)S(1)} %dynamic-slice_bitcast_fusion.16, f32[512,14]{0,1:T(8,128)S(1)} %dynamic-slice_bitcast_fusion.17), kind=kOutput, calls=%fused_computation.40.clone.1 | convolution fusion | flops 706478080 | bytes 2454016 | tf_op jit(solution)/shard_map/while/body/eval_jaxpr/rbk,bck->rc/dot_general | solution.py:33
  84.2 1.2 broadcast.138.clone
  85.4 7.3 %while.66 = (s32[]{:T(128)}, f32[2,512,384]{2,1,0:T(8,128)}, f32[2,16,512]{2,1,0:T(8,128)S(1)}, f32[2,512,128]{2,1,0:T(8,128)S(1)}, bf16[16,384,128]{2,1,0:T(8,128)(2,1)}, /*index=5*/s32[]{:T(128)}) while((s32[]{:T(128)}, f32[2,512,384]{2,1,0:T(8,128)}, f32[2,16,512]{2,1,0:T(8,128)S(1)}, f32[2,512,128]{2,1,0:T(8,128)S(1)}, ...), condition=%wide.region_8.9_spmd, body=%wide.region_7.8_spmd.sunk | while | flops 807403520 | bytes 3244621 | solution.py:35
  85.5 3.6 %fusion.104 = f32[2,512,384]{2,1,0:T(8,128)} fusion(f32[2,512,384]{2,1,0:T(8,128)} %get-tuple-element.675, s32[]{:T(128)} %get-tuple-element.674, bf16[16,384,128]{2,1,0:T(8,128)(2,1)} %get-tuple-element.684, f32[512,128]{1,0:T(8,128)S(1)} %dynamic-slice_bitcast_fusion.14, f32[512,16]{0,1:T(8,128)S(1)} %dynamic-slice_bitcast_fusion.15), kind=kOutput, calls=%fused_computation.32.clone.1 | convolution fusion | flops 807403520 | bytes 2654720 | tf_op jit(solution)/shard_map/while/body/eval_jaxpr/rbk,bck->rc/dot_general | solution.py:33
  89.1 3.6 %fusion.104 = f32[2,512,384]{2,1,0:T(8,128)} fusion(f32[2,512,384]{2,1,0:T(8,128)} %get-tuple-element.675, s32[]{:T(128)} %get-tuple-element.674, bf16[16,384,128]{2,1,0:T(8,128)(2,1)} %get-tuple-element.684, f32[512,128]{1,0:T(8,128)S(1)} %dynamic-slice_bitcast_fusion.14, f32[512,16]{0,1:T(8,128)S(1)} %dynamic-slice_bitcast_fusion.15), kind=kOutput, calls=%fused_computation.32.clone.1 | convolution fusion | flops 807403520 | bytes 2654720 | tf_op jit(solution)/shard_map/while/body/eval_jaxpr/rbk,bck->rc/dot_general | solution.py:33
  92.7 3.2 %add.114 = f32[2,512,384]{2,1,0:T(8,128)} add(f32[2,512,384]{2,1,0:T(8,128)} %get-tuple-element.193, f32[2,512,384]{2,1,0:T(8,128)} %get-tuple-element.194) | non-fusion elementwise | flops 393216 | bytes 4718592 | tf_op jit(solution)/shard_map/add | solution.py:114
  95.9 7.8 %all-to-all-done = bf16[2048,3,128]{2,1,0:T(4,128)(2,1)} async-done(((bf16[2048,3,128]{2,1,0:T(4,128)(2,1)}), bf16[2048,3,128]{2,1,0:T(4,128)(2,1)}, u32[]{:S(2)}, u32[]{:S(2)}) %all-to-all-start) | async-done | bytes 1572896 | tf_op jit(solution)/shard_map/all_to_all | solution.py:98
  103.7 4.1 %copy.26 = bf16[2048,3,128]{0,2,1:T(8,128)(2,1)} copy(bf16[2048,3,128]{2,1,0:T(4,128)(2,1)} %all-to-all-done) | data formatting | bytes 3145728 | tf_op jit(solution)/shard_map/all_to_all | solution.py:98
  107.8 1.9 copy.27
  109.7 5.0 %gather_fusion.1 = bf16[1024,384]{1,0:T(8,128)(2,1)} fusion(bf16[2048,384]{1,0:T(8,128)(2,1)S(1)} %copy.27, s32[1024]{0:T(1024)S(1)} %broadcast_clamp_fusion.4), kind=kCustom, calls=%fused_computation.1 | custom fusion | bytes 1576960 | tf_op jit(solution)/shard_map/gather | solution.py:103
  114.7 5.0 %gather_fusion.2 = bf16[1024,384]{1,0:T(8,128)(2,1)} fusion(bf16[2048,384]{1,0:T(8,128)(2,1)S(1)} %copy.27, s32[1024]{0:T(1024)S(1)} %broadcast_clamp_fusion.3), kind=kCustom, calls=%fused_computation.2 | custom fusion | bytes 1576960 | tf_op jit(solution)/shard_map/gather | solution.py:104
  119.7 2.7 fusion.58
  122.5 13.8 %while.65 = (s32[]{:T(128)}, f32[2,512,128]{2,1,0:T(8,128)S(1)}, bf16[2,14,512]{2,1,0:T(8,128)(2,1)S(1)}, bf16[2,512,384]{2,1,0:T(8,128)(2,1)}, bf16[14,384,128]{2,1,0:T(8,128)(2,1)}, /*index=5*/s32[]{:T(128)}) while((s32[]{:T(128)}, f32[2,512,128]{2,1,0:T(8,128)S(1)}, bf16[2,14,512]{2,1,0:T(8,128)(2,1)S(1)}, bf16[2,512,384]{2,1,0:T(8,128)(2,1)}, ...), condition=%wide.region_3.4_spmd, body=%wide.region_2.3_spmd.sunk | while | flops 706478080 | bytes 6298189 | solution.py:22
  122.5 3.8 %fusion.101 = bf16[512,14,128]{2,0,1:T(8,128)(2,1)} fusion(bf16[14,384,128]{2,1,0:T(8,128)(2,1)} %get-tuple-element.642, bf16[2,512,384]{2,1,0:T(8,128)(2,1)} %get-tuple-element.641, s32[]{:T(128)} %get-tuple-element.632), kind=kOutput, calls=%fused_computation.21.clone.1 | convolution fusion | flops 704643072 | bytes 3604992 | tf_op jit(solution)/shard_map/while/body/eval_jaxpr/rc,bck->rbk/dot_general | solution.py:19
  126.3 0.2 copy.55
  126.5 2.8 fusion.102
  129.4 3.8 %fusion.101 = bf16[512,14,128]{2,0,1:T(8,128)(2,1)} fusion(bf16[14,384,128]{2,1,0:T(8,128)(2,1)} %get-tuple-element.642, bf16[2,512,384]{2,1,0:T(8,128)(2,1)} %get-tuple-element.641, s32[]{:T(128)} %get-tuple-element.632), kind=kOutput, calls=%fused_computation.21.clone.1 | convolution fusion | flops 704643072 | bytes 3604992 | tf_op jit(solution)/shard_map/while/body/eval_jaxpr/rc,bck->rbk/dot_general | solution.py:19
  133.2 0.2 copy.55
  133.4 2.8 fusion.102
  136.3 15.0 %while.64 = (s32[]{:T(128)}, f32[2,512,128]{2,1,0:T(8,128)S(1)}, bf16[2,16,512]{2,1,0:T(8,128)(2,1)S(1)}, bf16[2,512,384]{2,1,0:T(8,128)(2,1)}, bf16[16,384,128]{2,1,0:T(8,128)(2,1)}, /*index=5*/s32[]{:T(128)}) while((s32[]{:T(128)}, f32[2,512,128]{2,1,0:T(8,128)S(1)}, bf16[2,16,512]{2,1,0:T(8,128)(2,1)S(1)}, bf16[2,512,384]{2,1,0:T(8,128)(2,1)}, ...), condition=%wide.region_1.2_spmd, body=%wide.region_0.1_spmd.sunk | while | flops 807403520 | bytes 7029325 | solution.py:22
  136.5 4.2 %fusion.95 = bf16[512,16,128]{2,0,1:T(8,128)(2,1)} fusion(bf16[16,384,128]{2,1,0:T(8,128)(2,1)} %get-tuple-element.624, bf16[2,512,384]{2,1,0:T(8,128)(2,1)} %get-tuple-element.623, s32[]{:T(128)} %get-tuple-element.614), kind=kOutput, calls=%fused_computation.13.clone.1 | convolution fusion | flops 805306368 | bytes 4063744 | tf_op jit(solution)/shard_map/while/body/eval_jaxpr/rc,bck->rbk/dot_general | solution.py:19
  140.7 0.2 copy.53
  140.8 3.0 %fusion.96 = f32[512,1,128]{2,1,0:T(1,128)S(1)} fusion(bf16[16,512,1]{0,2,1:T(2,128)(2,1)S(1)} %copy.53, bf16[512,16,128]{2,0,1:T(8,128)(2,1)} %fusion.95), kind=kOutput, calls=%fused_computation.11.clone.1 | convolution fusion | flops 2097152 | bytes 2375680 | tf_op jit(solution)/shard_map/while/body/eval_jaxpr/br,rbk->rk/dot_general | solution.py:20
  143.9 4.2 %fusion.95 = bf16[512,16,128]{2,0,1:T(8,128)(2,1)} fusion(bf16[16,384,128]{2,1,0:T(8,128)(2,1)} %get-tuple-element.624, bf16[2,512,384]{2,1,0:T(8,128)(2,1)} %get-tuple-element.623, s32[]{:T(128)} %get-tuple-element.614), kind=kOutput, calls=%fused_computation.13.clone.1 | convolution fusion | flops 805306368 | bytes 4063744 | tf_op jit(solution)/shard_map/while/body/eval_jaxpr/rc,bck->rbk/dot_general | solution.py:19
  148.1 0.2 copy.53
  148.3 3.0 %fusion.96 = f32[512,1,128]{2,1,0:T(1,128)S(1)} fusion(bf16[16,512,1]{0,2,1:T(2,128)(2,1)S(1)} %copy.53, bf16[512,16,128]{2,0,1:T(8,128)(2,1)} %fusion.95), kind=kOutput, calls=%fused_computation.11.clone.1 | convolution fusion | flops 2097152 | bytes 2375680 | tf_op jit(solution)/shard_map/while/body/eval_jaxpr/br,rbk->rk/dot_general | solution.py:20
  151.3 0.1 add.108
  151.4 5.5 %gather_fusion.3 = f32[2048,128]{1,0:T(8,128)S(1)} fusion(f32[1024,128]{1,0:T(8,128)S(1)} %bitcast.151, s32[2048]{0:T(1024)S(1)} %broadcast_clamp_fusion.1), kind=kCustom, calls=%fused_computation.3 | custom fusion | bytes 2105344 | tf_op jit(solution)/shard_map/gather | solution.py:116
  156.9 7.6 %gather_fusion.4 = f32[2048,128]{1,0:T(8,128)} fusion(f32[1024,128]{1,0:T(8,128)S(1)} %bitcast.152, s32[2048]{0:T(1024)S(1)} %broadcast_clamp_fusion), kind=kCustom, calls=%fused_computation.4 | custom fusion | bytes 2105344 | tf_op jit(solution)/shard_map/gather | solution.py:117
  164.5 2.6 add_convert_fusion
  167.1 3.9 %all-to-all-start.1 = ((bf16[32,64,128]{2,1,0:T(8,128)(2,1)}), bf16[32,64,128]{2,1,0:T(8,128)(2,1)S(1)}, u32[]{:S(2)}, u32[]{:S(2)}) async-start(bf16[32,64,128]{2,1,0:T(8,128)(2,1)} %add_convert_fusion), calls=%async_computation.1 | async-start | bytes 1048576 | tf_op jit(solution)/shard_map/all_to_all | solution.py:124
  171.1 21.3 %while.69 = (s32[]{:T(128)}, f32[2048,384]{1,0:T(8,128)}, s32[2,512]{1,0:T(2,128)S(1)}, f32[2,512]{1,0:T(2,128)S(1)}, s32[2,512]{1,0:T(2,128)S(1)}, /*index=5*/f32[2,512,384]{2,1,0:T(8,128)}, s32[]{:T(128)}, s32[]{:T(128)}) while((s32[]{:T(128)}, f32[2048,384]{1,0:T(8,128)}, s32[2,512]{1,0:T(2,128)S(1)}, ...), condition=%wide.region_12.13_spmd.clone.clone, body=%wide.region_11.12_spmd.clone.clone.sunk | while | flops 4838654464 | bytes 7103079 | solution.py:68
  171.2 10.4 %select_add_fusion.2 = f32[2048,384]{1,0:T(8,128)} fusion(f32[2048,384]{1,0:T(8,128)} %get-tuple-element.713, f32[512]{0:T(512)S(1)} %broadcast_subtract_fusion.7, s32[512]{0:T(512)S(1)} %bitcast.172, f32[512]{0:T(512)S(1)} %bitcast.169, s32[512]{0:T(512)S(1)} %bitcast.173, pred[]{:T(512)S(6)} %compare.7, f32[2,512,384]{2,1,0:T(8,128)} %get-tuple-element.725, ...), kind=kOutput, calls=%fused_computation.69.clone.1 | convolution fusion | flops 4838653952 | bytes 7086593 | tf_op jit(solution)/shard_map/while/body/eval_jaxpr/nt,nw->tw/dot_general | solution.py:52
  181.6 10.8 %select_add_fusion.2 = f32[2048,384]{1,0:T(8,128)} fusion(f32[2048,384]{1,0:T(8,128)} %get-tuple-element.713, f32[512]{0:T(512)S(1)} %broadcast_subtract_fusion.7, s32[512]{0:T(512)S(1)} %bitcast.172, f32[512]{0:T(512)S(1)} %bitcast.169, s32[512]{0:T(512)S(1)} %bitcast.173, pred[]{:T(512)S(6)} %compare.7, f32[2,512,384]{2,1,0:T(8,128)} %get-tuple-element.725, ...), kind=kOutput, calls=%fused_computation.69.clone.1 | convolution fusion | flops 4838653952 | bytes 7086593 | tf_op jit(solution)/shard_map/while/body/eval_jaxpr/nt,nw->tw/dot_general | solution.py:52
  192.4 3.0 %copy.33 = bf16[2048,384]{0,1:T(8,128)(2,1)} copy(f32[2048,384]{1,0:T(8,128)} %get-tuple-element.195) | data formatting | bytes 4718592 | tf_op jit(solution)/shard_map/while | solution.py:68
  195.4 4.1 %copy.34 = bf16[2048,3,128]{2,1,0:T(4,128)(2,1)} copy(bf16[2048,3,128]{0,2,1:T(8,128)(2,1)} %bitcast.158) | data formatting | bytes 3145728 | tf_op jit(solution)/shard_map/reshape | solution.py:122
  199.6 6.0 %all-to-all-start.3 = ((bf16[2048,3,128]{2,1,0:T(4,128)(2,1)}), bf16[2048,3,128]{2,1,0:T(4,128)(2,1)}, u32[]{:S(2)}, u32[]{:S(2)}) async-start(bf16[2048,3,128]{2,1,0:T(4,128)(2,1)} %copy.34), calls=%async_computation.3 | async-start | bytes 4194304 | tf_op jit(solution)/shard_map/all_to_all | solution.py:125
  205.5 8.0 %scatter_custom_fusion = s32[2048]{0:T(1024)S(1)} fusion(s32[2048]{0:T(1024)S(1)} %bitcast.175, s32[2048]{0:T(1024)S(1)} %iota.13, s32[]{:T(128)} %constant.84.clone.1), kind=kCustom, calls=%fused_computation.102 | custom fusion | bytes 8196 | tf_op jit(solution)/shard_map/scatter | solution.py:128
  213.6 8.1 %gather_fusion.5 = bf16[2048,128]{1,0:T(8,128)(2,1)} fusion(bf16[2048,128]{1,0:T(8,128)(2,1)S(1)} %bitcast.153, s32[2048]{0:T(1024)S(1)} %fusion.59), kind=kCustom, calls=%fused_computation.5 | custom fusion | bytes 1056768 | tf_op jit(solution)/shard_map/gather | solution.py:130
  221.7 32.6 %all-to-all-done.3 = bf16[2048,3,128]{2,1,0:T(4,128)(2,1)} async-done(((bf16[2048,3,128]{2,1,0:T(4,128)(2,1)}), bf16[2048,3,128]{2,1,0:T(4,128)(2,1)}, u32[]{:S(2)}, u32[]{:S(2)}) %all-to-all-start.3) | async-done | bytes 1572896 | tf_op jit(solution)/shard_map/all_to_all | solution.py:125
  254.2 16.1 %gather_fusion.7 = bf16[2048,3,128]{2,1,0:T(4,128)(2,1)} fusion(bf16[2048,3,128]{2,1,0:T(4,128)(2,1)} %all-to-all-done.3, s32[2048]{0:T(1024)S(1)} %fusion.59), kind=kCustom, calls=%fused_computation.7 | custom fusion | bytes 3153920 | tf_op jit(solution)/shard_map/gather | solution.py:131
  270.3 3.0 %copy.35 = bf16[2048,3,128]{2,0,1:T(8,128)(2,1)} copy(bf16[2048,3,128]{2,1,0:T(4,128)(2,1)} %gather_fusion.7) | data formatting | bytes 3145728
  (83 shorter events, 0.8 us)
Async XLA Ops:
  7.2 18.7 %copy-start = (bf16[2048,3,128]{2,0,1:T(8,128)(2,1)S(1)}, bf16[2048,3,128]{2,0,1:T(8,128)(2,1)}, u32[]{:S(2)}) copy-start(bf16[2048,3,128]{2,0,1:T(8,128)(2,1)} %param.24) | copy-start | bytes 4718596
  7.2 68.9 %all-gather.5.cloned.1.call-start = ((), (), s32[]{:S(2)}) async-start(), calls=%async_computation.5 | async-start | bytes 1548288 | tf_op jit(solution)/shard_map/all_gather | solution.py:88
  8.6 17.0 %copy-start.6 = (f32[1024]{0:T(1024)S(1)}, f32[1024]{0:T(1024)}, u32[]{:S(2)}) copy-start(f32[1024]{0:T(1024)} %param.28) | copy-start | bytes 12292
  8.6 17.0 %copy-start.1 = (f32[2048]{0:T(1024)S(1)}, f32[2048]{0:T(1024)}, u32[]{:S(2)}) copy-start(f32[2048]{0:T(1024)} %param.30) | copy-start | bytes 24580
  8.7 17.1 %copy-start.4 = (s32[2,2048]{1,0:T(2,128)S(1)}, s32[2,2048]{1,0:T(2,128)}, u32[]{:S(2)}) copy-start(s32[2,2048]{1,0:T(2,128)} %param.29) | copy-start | bytes 49156
  17.5 31.4 %all-to-all-start.2 = ((bf16[32,64,128]{2,1,0:T(8,128)(2,1)}), bf16[32,64,128]{2,1,0:T(8,128)(2,1)S(1)}, u32[]{:S(2)}, u32[]{:S(2)}) async-start(bf16[32,64,128]{2,1,0:T(8,128)(2,1)} %bitcast.45), calls=%async_computation.2 | async-start | bytes 1048576 | tf_op jit(solution)/shard_map/all_to_all | solution.py:99
  24.8 59.3 %all-gather.3.cloned.1.call-start = ((), (), s32[]{:S(2)}) async-start(), calls=%async_computation.4 | async-start | bytes 1769472 | tf_op jit(solution)/shard_map/all_gather | solution.py:87
  44.2 4.2 %copy-start.5 = (s32[2,1024]{1,0:T(2,128)S(1)}, s32[2,1024]{1,0:T(2,128)}, u32[]{:S(2)}) copy-start(s32[2,1024]{1,0:T(2,128)} %param.27) | copy-start | bytes 24580
  44.2 4.3 %copy-start.7 = (s32[1024]{0:T(1024)S(1)}, s32[1024]{0:T(1024)}, u32[]{:S(2)}) copy-start(s32[1024]{0:T(1024)} %param.33) | copy-start | bytes 12292
  44.2 4.3 %copy-start.2 = (f32[14,1024]{1,0:T(8,128)S(1)}, f32[14,1024]{1,0:T(8,128)}, u32[]{:S(2)}) copy-start(f32[14,1024]{1,0:T(8,128)} %param.32) | copy-start | bytes 172036
  44.2 4.4 %copy-start.3 = (f32[16,1024]{1,0:T(8,128)S(1)}, f32[16,1024]{1,0:T(8,128)}, u32[]{:S(2)}) copy-start(f32[16,1024]{1,0:T(8,128)} %param.31) | copy-start | bytes 196612
  48.9 54.8 %all-to-all-start = ((bf16[2048,3,128]{2,1,0:T(4,128)(2,1)}), bf16[2048,3,128]{2,1,0:T(4,128)(2,1)}, u32[]{:S(2)}, u32[]{:S(2)}) async-start(bf16[2048,3,128]{2,1,0:T(4,128)(2,1)} %copy.25), calls=%async_computation | async-start | bytes 4194304 | tf_op jit(solution)/shard_map/all_to_all | solution.py:98
  167.1 32.4 %all-to-all-start.1 = ((bf16[32,64,128]{2,1,0:T(8,128)(2,1)}), bf16[32,64,128]{2,1,0:T(8,128)(2,1)S(1)}, u32[]{:S(2)}, u32[]{:S(2)}) async-start(bf16[32,64,128]{2,1,0:T(8,128)(2,1)} %add_convert_fusion), calls=%async_computation.1 | async-start | bytes 1048576 | tf_op jit(solution)/shard_map/all_to_all | solution.py:124
  199.6 54.7 %all-to-all-start.3 = ((bf16[2048,3,128]{2,1,0:T(4,128)(2,1)}), bf16[2048,3,128]{2,1,0:T(4,128)(2,1)}, u32[]{:S(2)}, u32[]{:S(2)}) async-start(bf16[2048,3,128]{2,1,0:T(4,128)(2,1)} %copy.34), calls=%async_computation.3 | async-start | bytes 4194304 | tf_op jit(solution)/shard_map/all_to_all | solution.py:125
Sparse Core Ops, SparseCore 0:
  9.9 29.9 all-gather.4
  41.8 35.1 all-gather.2
where the time goes:
time: 281 us; the launch traced here: 280 us
  local copies, waits for them, and re-layouts  107 us (38%)
  matrix products  82.5 us (29%)
  waiting for transfers between devices  41.8 us (15%)
  starting transfers between devices  23.5 us (8%)
  between operations  14.4 us (5%)
  other arithmetic  10.5 us (4%)
    dot_general x6, matrix products, one_block(): jnp.einsum('nt,nw->tw', table, rows, precision=lax.Precision.HIGHEST, pre...  40.8 us
    all_to_all x1, waiting for transfers between devices, local(): lax.all_to_all(gradient_rad, ('lat', 'lon'), split_axis=0, concat_axis=0,...  32.6 us
    gather x2, local copies, waits for them, and re-layouts, local(): sent_fields = increments[order_map]  22.6 us
    gather x1, local copies, waits for them, and re-layouts, local(): gradient = back_gradient[inverse_map]  16.1 us
    dot_general x4, matrix products, one_block(): jnp.einsum('rc,bck->rbk', pair[0], band_table, preferred_element_type=jnp...  16 us
    dot_general x4, matrix products, one_block(): jnp.einsum('rbk,bck->rc', lifted, band_table, preferred_element_type=jnp....  14 us
    dot_general x4, matrix products, one_block(): return jnp.einsum('br,rbk->rk', pair[1], product)  11.6 us
    gather x1, local copies, waits for them, and re-layouts, local(): sent_cotangent = cotangent[order_map]  8.84 us
  transfers between devices with their start and end apart: 6, of which 2 were waited for; matrix products, arithmetic and copies ran while one was open for 42% of the time, Pallas kernels for 0%

commit v1 on v0

v1 whole, which is shorter than its diff:
```python
import jax
import jax.numpy as jnp
from jax import lax
from jax.experimental import pallas as pl
from jax.experimental.pallas import tpu as pltpu
from jax.sharding import PartitionSpec as P

BLOCK = 256


def lane_iota(rows, width):
    return lax.broadcasted_iota(jnp.int32, (rows, width), 1)


def row_iota(rows, width, start):
    return lax.broadcasted_iota(jnp.int32, (rows, width), 0) + start


def pick(hit):
    return jnp.where(hit, 1.0, 0.0).astype(jnp.bfloat16)


def blend(hit_first, hit_second, share):
    first = jnp.where(hit_first, share, 0.0)
    second = jnp.where(hit_second, 1.0 - share, 0.0)
    return (first + second).astype(jnp.bfloat16)


def dot(left, right):
    return lax.dot_general(left, right, (((1,), (0,)), ((), ())), preferred_element_type=jnp.float32)


def send_kernel(perm_ref, inc_ref, cot_ref, cot_out, fields_out, stacked):
    var_count, col_count, width = inc_ref.shape
    segment = fields_out.shape[2]
    per_block = BLOCK // segment
    stacked[:, pl.ds(0, width)] = cot_ref[...]
    for v in range(var_count):
        stacked[:, pl.ds((v + 1) * width, width)] = inc_ref[v]

    @pl.loop(0, col_count // BLOCK)
    def one(step):
        rows = pl.ds(pl.multiple_of(step * BLOCK, BLOCK), BLOCK)
        column = jnp.transpose(jnp.broadcast_to(perm_ref[:, rows], (8, BLOCK)))[:, 0:1]
        table = pick(column == lane_iota(BLOCK, col_count))
        moved = dot(table, stacked[...]).astype(jnp.bfloat16)
        cot_out[rows, :] = moved[:, :width]
        for v in range(var_count):
            piece = moved[:, (v + 1) * width : (v + 2) * width]
            fields_out[pl.ds(step * per_block, per_block), v] = piece.reshape(per_block, segment, width)


def lay_tables(lw_ref, sw_ref, wide):
    at = 0
    for ref in (lw_ref, sw_ref):
        for b in range(ref.shape[0]):
            wide[:, pl.ds(at, ref.shape[3])] = ref[b].reshape(wide.shape[0], ref.shape[3])
            at += ref.shape[3]


def adjoint_kernel(cot_ref, back_ref, back_w, scale_ref, lw_ref, sw_ref, coarse_ref, coarse_w, grad_out, wide_out, adj):
    lay_tables(lw_ref, sw_ref, wide_out)
    row_count = scale_ref.shape[1]
    col_count, width = cot_ref.shape
    band_count = lw_ref.shape[0] + sw_ref.shape[0]
    var_count, segment = grad_out.shape[1], grad_out.shape[2]
    per_block = BLOCK // segment

    @pl.loop(0, row_count // BLOCK)
    def one(step):
        start = pl.multiple_of(step * BLOCK, BLOCK)
        rows = pl.ds(start, BLOCK)
        spot = row_iota(BLOCK, col_count, start)
        table = blend(back_ref[0:1, :] == spot, back_ref[1:2, :] == spot, back_w[...])
        coarse = dot(table, cot_ref[...])
        scale = jnp.transpose(scale_ref[:, rows])
        lifted = jnp.concatenate([(scale[:, b : b + 1] * coarse).astype(jnp.bfloat16) for b in range(band_count)], axis=1)
        out = lax.dot_general(lifted, wide_out[...], (((1,), (1,)), ((), ())), preferred_element_type=jnp.float32)
        adj[rows, :] = out.astype(jnp.bfloat16)

    @pl.loop(0, col_count // BLOCK)
    def two(step):
        spot = row_iota(BLOCK, row_count, step * BLOCK)
        table = blend(coarse_ref[0:1, :] == spot, coarse_ref[1:2, :] == spot, coarse_w[...])
        moved = dot(table, adj[...]).astype(jnp.bfloat16)
        for v in range(var_count):
            piece = moved[:, v * width : (v + 1) * width]
            grad_out[pl.ds(step * per_block, per_block), v] = piece.reshape(per_block, segment, width)


def column_of(values):
    return jnp.transpose(jnp.broadcast_to(values, (8, values.shape[1])))[:, 0:1]


def heating_kernel(fields_ref, back_ref, back_w, scale_ref, wide_ref, coarse_ref, coarse_w, tend_out, flat, heat):
    devices, var_count, segment, width = fields_ref.shape
    col_count = devices * segment
    row_count = scale_ref.shape[1]
    band_count = wide_ref.shape[1] // width
    for v in range(var_count):
        flat[:, pl.ds(v * width, width)] = fields_ref[:, v].reshape(col_count, width)

    @pl.loop(0, row_count // BLOCK)
    def one(step):
        rows = pl.ds(pl.multiple_of(step * BLOCK, BLOCK), BLOCK)
        spot = lane_iota(BLOCK, col_count)
        first, second = column_of(coarse_ref[0:1, rows]), column_of(coarse_ref[1:2, rows])
        table = blend(first == spot, second == spot, column_of(coarse_w[:, rows]))
        coarse = dot(table, flat[...]).astype(jnp.bfloat16)
        scale = jnp.transpose(scale_ref[:, rows])
        total = jnp.zeros((BLOCK, width), jnp.float32)
        for b in range(0, band_count, 2):
            pair = dot(coarse, wide_ref[:, b * width : (b + 2) * width])
            total = total + scale[:, b : b + 1] * pair[:, :width] + scale[:, b + 1 : b + 2] * pair[:, width:]
        heat[rows, :] = total.astype(jnp.bfloat16)

    @pl.loop(0, col_count // BLOCK)
    def two(step):
        rows = pl.ds(pl.multiple_of(step * BLOCK, BLOCK), BLOCK)
        spot = lane_iota(BLOCK, row_count)
        first, second = column_of(back_ref[0:1, rows]), column_of(back_ref[1:2, rows])
        table = blend(first == spot, second == spot, column_of(back_w[:, rows]))
        tend_out[rows, :] = dot(table, heat[...]).astype(jnp.bfloat16)


def restore_kernel(perm_ref, tend_ref, grad_ref, tend_out, grad_out, stacked):
    devices, var_count, segment, width = grad_ref.shape
    col_count = devices * segment
    stacked[:, pl.ds(0, width)] = tend_ref[...]
    for v in range(var_count):
        stacked[:, pl.ds((v + 1) * width, width)] = grad_ref[:, v].reshape(col_count, width)

    @pl.loop(0, col_count // BLOCK)
    def one(step):
        rows = pl.ds(pl.multiple_of(step * BLOCK, BLOCK), BLOCK)
        table = pick(perm_ref[...] == row_iota(BLOCK, col_count, step * BLOCK))
        moved = dot(table, stacked[...]).astype(jnp.bfloat16)
        tend_out[rows, :] = moved[:, :width]
        for v in range(var_count):
            grad_out[v, rows, :] = moved[:, (v + 1) * width : (v + 2) * width]


def run(kernel, outs, scratch, flops, args):
    shapes = [jax.ShapeDtypeStruct(shape, jnp.bfloat16) for shape in outs]
    vmem = pl.BlockSpec(memory_space=pltpu.VMEM)
    return pl.pallas_call(
        kernel,
        out_shape=shapes,
        in_specs=[vmem] * len(args),
        out_specs=[vmem] * len(outs),
        scratch_shapes=[pltpu.VMEM(shape, jnp.bfloat16) for shape in scratch],
        compiler_params=pltpu.CompilerParams(vmem_limit_bytes=56 * 1024 * 1024),
        cost_estimate=pl.CostEstimate(flops=flops, bytes_accessed=4 << 20, transcendentals=0),
    )(*args)


def local(
    increments,
    cotangent,
    owner_perm,
    coarse_index,
    coarse_weight,
    back_index,
    back_weight,
    lw_scale,
    sw_scale,
    sunlit,
    lw_table,
    sw_table,
    *,
    devices,
):
    axes = ("lat", "lon")
    sw_full = lax.all_gather(sw_table, "lon", axis=2, tiled=True)
    lw_full = lax.all_gather(lw_table, "lon", axis=2, tiled=True)
    col_count, var_count, width = increments.shape
    row_count = coarse_weight.shape[0]
    segment = col_count // devices
    split = (devices, var_count, segment, width)
    flat_width = var_count * width
    bands = lw_table.shape[0] + sw_table.shape[0]
    planes = jnp.transpose(increments, (1, 0, 2))
    stack = (col_count, (var_count + 1) * width)
    move_cost = 2 * col_count * stack[0] * stack[1]
    sent_cot, sent_fields = run(
        send_kernel, [(col_count, width), split], [stack], move_cost, (owner_perm, planes, cotangent)
    )
    cot_rad = lax.all_to_all(sent_cot, axes, split_axis=0, concat_axis=0, tiled=True)
    fields = lax.all_to_all(sent_fields, axes, split_axis=0, concat_axis=0, tiled=True)
    scale = jnp.concatenate([lw_scale, sw_scale * sunlit.astype(jnp.float32)[None, :], jnp.zeros((-bands % 8, row_count), jnp.float32)])
    back_w, coarse_w = back_weight[None, :], coarse_weight[None, :]
    band_cost = 3 * row_count * bands * flat_width * width
    sent_grad, wide = run(
        adjoint_kernel,
        [split, (flat_width, bands * width)],
        [(row_count, flat_width)],
        band_cost,
        (cot_rad, back_index, back_w, scale, lw_full, sw_full, coarse_index, coarse_w),
    )
    back_grad = lax.all_to_all(sent_grad, axes, split_axis=0, concat_axis=0, tiled=True)
    (sent_tend,) = run(
        heating_kernel,
        [(col_count, width)],
        [(col_count, flat_width), (row_count, width)],
        band_cost,
        (fields, back_index, back_w, scale, wide, coarse_index, coarse_w),
    )
    back_tend = lax.all_to_all(sent_tend, axes, split_axis=0, concat_axis=0, tiled=True)
    tendency, gradient = run(
        restore_kernel,
        [(col_count, width), (var_count, col_count, width)],
        [stack],
        move_cost,
        (owner_perm, back_tend, back_grad),
    )
    return (tendency, jnp.transpose(gradient, (1, 0, 2)))


def solution(mesh):
    in_specs = (
        P(("lat", "lon"), None, None),
        P(("lat", "lon"), None),
        P(("lat", "lon"), None),
        P(None, ("lat", "lon")),
        P(("lat", "lon")),
        P(None, ("lat", "lon")),
        P(("lat", "lon")),
        P(None, ("lat", "lon")),
        P(None, ("lat", "lon")),
        P(("lat", "lon")),
        P(None, None, "lon", None),
        P(None, None, "lon", None),
    )
    out_specs = (P(("lat", "lon"), None), P(("lat", "lon"), None, None))
    devices = mesh.shape["lat"] * mesh.shape["lon"]

    def body(*args):
        return local(*args, devices=devices)

    return jax.shard_map(body, mesh=mesh, in_specs=in_specs, out_specs=out_specs, check_vma=False)
```

time: 281 us -> 189 us (0.67)
  local copies, waits for them, and re-layouts: 107 us -> 2.01 us
  matrix products: 82.5 us -> 0 us
  blocking collectives: 0 us -> 62.4 us
  Pallas kernels: 0 us -> 51.8 us
  starting transfers between devices: 23.5 us -> 10.4 us
  other arithmetic: 10.5 us -> 0.74 us
  waiting for transfers between devices: 41.8 us -> 47.1 us
    dot_general x18 -> x0, matrix products: 82.5 us -> none  [the longest x6 40.8 us: one_block(): jnp.einsum('nt,nw->tw', table, rows, precision=lax.Precision.HIGHEST, pre...]
    gather x9 -> x0, local copies, waits for them, and re-layouts: 78.7 us -> none  [the longest x2 22.6 us: local(): sent_fields = increments[order_map]]
    all_to_all x0 -> x2, blocking collectives: none -> 62.4 us  [the longest x1 41 us: local(): lax.all_to_all(sent_grad, axes, split_axis=0, concat_axis=0, tiled=True)]
    pallas_call x0 -> x4, Pallas kernels: none -> 51.8 us  [run(): pl.pallas_call(kernel, out_shape=shapes, in_specs=[vmem] * len(args), out...]
    all_gather x2, waiting for transfers between devices: 0.02 us -> 30.9 us  [the longest x1 30.9 us: local(): lw_full = lax.all_gather(lw_table, 'lon', axis=2, tiled=True)]
    all_to_all x4 -> x2, waiting for transfers between devices: 40.4 us -> 14.9 us  [the longest x1 14.9 us: local(): lax.all_to_all(sent_cot, axes, split_axis=0, concat_axis=0, tiled=True)]
    all_to_all x4 -> x2, starting transfers between devices: 23.4 us -> 10.3 us  [the longest x1 7.31 us: local(): lax.all_to_all(sent_cot, axes, split_axis=0, concat_axis=0, tiled=True)]
    scatter x1 -> x0, local copies, waits for them, and re-layouts: 8.05 us -> none  [local(): jnp.zeros((col_count,), jnp.int32).at[order_map]]
  transfers between devices with their start and end apart: 6 -> 4, of which waited for: 2 -> 2; matrix products, arithmetic and copies ran while one was open for 42% -> 0% of each run, Pallas kernels for 0% -> 13%
where the time goes in v1:
time: 189 us
  blocking collectives  62.4 us (33%)
  Pallas kernels  51.8 us (27%)
  waiting for transfers between devices  47.1 us (25%)
  between operations  14.1 us (7%)
  starting transfers between devices  10.4 us (6%)
  local copies, waits for them, and re-layouts  2.01 us (1%)
    pallas_call x4, Pallas kernels, run(): pl.pallas_call(kernel, out_shape=shapes, in_specs=[vmem] * len(args), out...  51.8 us
    all_to_all x1, blocking collectives, local(): lax.all_to_all(sent_grad, axes, split_axis=0, concat_axis=0, tiled=True)  41 us
    all_gather x1, waiting for transfers between devices, local(): lw_full = lax.all_gather(lw_table, 'lon', axis=2, tiled=True)  30.9 us
    all_to_all x1, blocking collectives, local(): lax.all_to_all(sent_tend, axes, split_axis=0, concat_axis=0, tiled=True)  21.4 us
    all_to_all x1, waiting for transfers between devices, local(): lax.all_to_all(sent_cot, axes, split_axis=0, concat_axis=0, tiled=True)  14.9 us
    all_to_all x1, starting transfers between devices, local(): lax.all_to_all(sent_cot, axes, split_axis=0, concat_axis=0, tiled=True)  7.31 us
  transfers between devices with their start and end apart: 4, of which 2 were waited for; matrix products, arithmetic and copies ran while one was open for 0% of the time, Pallas kernels for 13%

profile of v1, /device:TPU:0, one launch (start us, length us, event | category | flops | bytes accessed | tf_op | source)
XLA Modules:
  0.0 188.5 jit_solution(11032744515719424443)
XLA Ops:
  7.2 0.0 all-gather.5.cloned.1.call-start
  7.2 0.7 all-gather.5.cloned.1.call-update
  7.9 10.8 %shard_map.131 = (bf16[2048,128]{1,0:T(8,128)(2,1)}, bf16[32,3,64,128]{3,2,1,0:T(8,128)(2,1)}) custom-call(s32[1,2048]{1,0:T(1,128)} %perm_ref.3, bf16[3,2048,128]{2,1,0:T(8,128)(2,1)} %bitcast.12, bf16[2048,128]{1,0:T(8,128)(2,1)} %cot_ref.1), custom_call_target="tpu_custom_call" | custom-call | flops 4294967296 | bytes 4194304 | tf_op jit(solution)/shard_map/pallas_call | solution.py:146
  18.7 7.3 %all-to-all-start.1 = ((bf16[32,64,128]{2,1,0:T(8,128)(2,1)}), bf16[32,64,128]{2,1,0:T(8,128)(2,1)S(1)}, u32[]{:S(2)}, u32[]{:S(2)}) async-start(bf16[32,64,128]{2,1,0:T(8,128)(2,1)} %bitcast.9), calls=%async_computation.1 | async-start | bytes 1048576 | tf_op jit(solution)/shard_map/all_to_all | solution.py:188
  26.0 0.0 all-gather.3.cloned.1.call-start
  26.1 0.7 all-gather.3.cloned.1.call-update
  26.8 14.9 %all-to-all-done.1 = bf16[32,64,128]{2,1,0:T(8,128)(2,1)S(1)} async-done(((bf16[32,64,128]{2,1,0:T(8,128)(2,1)}), bf16[32,64,128]{2,1,0:T(8,128)(2,1)S(1)}, u32[]{:S(2)}, u32[]{:S(2)}) %all-to-all-start.1) | async-done | bytes 524320 | tf_op jit(solution)/shard_map/all_to_all | solution.py:188
  41.7 0.0 copy-start.2
  41.7 0.0 copy-start.5
  41.7 0.0 copy-start.3
  41.7 0.0 copy-start.4
  41.7 0.8 copy-done.2
  42.4 3.0 %all-to-all-start = ((bf16[32,3,64,128]{3,2,1,0:T(8,128)(2,1)}), bf16[32,3,64,128]{3,2,1,0:T(8,128)(2,1)S(1)}, u32[]{:S(2)}, u32[]{:S(2)}) async-start(bf16[32,3,64,128]{3,2,1,0:T(8,128)(2,1)} %get-tuple-element.8), calls=%async_computation | async-start | bytes 3145728 | tf_op jit(solution)/shard_map/all_to_all | solution.py:189
  45.4 0.0 copy-done.5
  45.5 0.1 pad.2.clone
  45.5 0.0 copy-done.3
  45.5 0.0 copy-done.4
  45.6 0.7 maximum_maximum_fusion.scale_ref
  46.3 0.0 all-gather.5.cloned.1.call-done.sw_ref
  46.3 30.9 %all-gather.3.cloned.1.call-done.lw_ref = bf16[16,3,128,128]{3,2,1,0:T(8,128)(2,1)} async-done(((bf16[16,3,16,128]{3,2,1,0:T(8,128)(2,1)}), bf16[16,3,128,128]{3,2,1,0:T(8,128)(2,1)}) %all-gather.3.cloned.1.call-update) | async-done | bytes 1572880 | tf_op jit(solution)/shard_map/all_gather | solution.py:175
  77.2 14.4 %shard_map.132 = (bf16[32,3,64,128]{3,2,1,0:T(8,128)(2,1)}, bf16[384,3840]{1,0:T(8,128)(2,1)}) custom-call(bf16[2048,128]{1,0:T(8,128)(2,1)} %bitcast.8, s32[2,2048]{1,0:T(2,128)} %back_ref.3, f32[1,2048]{1,0:T(1,128)} %bitcast.13, f32[32,1024]{1,0:T(8,128)} %maximum_maximum_fusion.scale_ref, bf16[16,3,128,128]{3,2,1,0:T(8,128)(2,1)} %all-gather.3.cloned.1.call-done.lw_ref, ...), custom_call_target="tpu_custom_call" | custom-call | flops 4529848320 | bytes 4194304 | tf_op jit(solution)/shard_map/pallas_call | solution.py:146
  91.6 0.0 all-to-all-done.fields_ref
  91.6 0.0 copy-start
  91.6 1.1 copy-done
  92.7 0.0 copy-start.1
  92.7 17.6 %shard_map.133 = bf16[2048,128]{1,0:T(8,128)(2,1)} custom-call(bf16[32,3,64,128]{3,2,1,0:T(8,128)(2,1)} %copy-done, s32[2,2048]{1,0:T(2,128)} %back_ref.3, f32[1,2048]{1,0:T(1,128)} %bitcast.14, f32[32,1024]{1,0:T(8,128)} %maximum_maximum_fusion.scale_ref, bf16[384,3840]{1,0:T(8,128)(2,1)} %get-tuple-element.10.wide_ref, s32[2,1024]{1,0:T(2,128)} %coarse_ref.3, ...), custom_call_target="tpu_custom_call" | custom-call | flops 4529848320 | bytes 4194304 | tf_op jit(solution)/shard_map/pallas_call | solution.py:146
  110.4 21.4 %all_to_all.32 = bf16[32,64,128]{2,1,0:T(8,128)(2,1)} all-to-all(bf16[32,64,128]{2,1,0:T(8,128)(2,1)} %bitcast.11), channel_id=1, replica_groups=mesh['lat'=4,'lon'=8] {'lat','lon'}, dimensions={0} | all-to-all | bytes 1048576 | tf_op jit(solution)/shard_map/all_to_all | solution.py:208
  131.8 0.0 copy-done.1
  131.8 41.0 %all_to_all.33.grad_ref = bf16[32,3,64,128]{3,2,1,0:T(8,128)(2,1)} all-to-all(bf16[32,3,64,128]{3,2,1,0:T(8,128)(2,1)S(1)} %copy-done.1), channel_id=1, replica_groups=mesh['lat'=4,'lon'=8] {'lat','lon'}, dimensions={0} | all-to-all | bytes 3145728 | tf_op jit(solution)/shard_map/all_to_all | solution.py:200
  172.8 8.9 %shard_map.134 = (bf16[2048,128]{1,0:T(8,128)(2,1)}, bf16[3,2048,128]{2,1,0:T(8,128)(2,1)}) custom-call(s32[1,2048]{1,0:T(1,128)} %perm_ref.3, bf16[2048,128]{1,0:T(8,128)(2,1)} %bitcast.10, bf16[32,3,64,128]{3,2,1,0:T(8,128)(2,1)} %all_to_all.33.grad_ref), custom_call_target="tpu_custom_call" | custom-call | flops 4294967296 | bytes 4194304 | tf_op jit(solution)/shard_map/pallas_call | solution.py:146
  (3 shorter events, 0.0 us)
Async XLA Ops:
  7.2 39.1 %all-gather.5.cloned.1.call-start = ((), (), s32[]{:S(2)}) async-start(), calls=%async_computation.5 | async-start | bytes 1548288 | tf_op jit(solution)/shard_map/all_gather | solution.py:174
  18.7 22.9 %all-to-all-start.1 = ((bf16[32,64,128]{2,1,0:T(8,128)(2,1)}), bf16[32,64,128]{2,1,0:T(8,128)(2,1)S(1)}, u32[]{:S(2)}, u32[]{:S(2)}) async-start(bf16[32,64,128]{2,1,0:T(8,128)(2,1)} %bitcast.9), calls=%async_computation.1 | async-start | bytes 1048576 | tf_op jit(solution)/shard_map/all_to_all | solution.py:188
  26.0 51.1 %all-gather.3.cloned.1.call-start = ((), (), s32[]{:S(2)}) async-start(), calls=%async_computation.4 | async-start | bytes 1769472 | tf_op jit(solution)/shard_map/all_gather | solution.py:175
  41.7 0.8 copy-start.2
  41.7 3.8 %copy-start.5 = (s32[1024]{0:T(1024)S(1)}, s32[1024]{0:T(1024)}, u32[]{:S(2)}) copy-start(s32[1024]{0:T(1024)} %param.21) | copy-start | bytes 12292
  41.7 3.9 %copy-start.3 = (f32[14,1024]{1,0:T(8,128)S(1)}, f32[14,1024]{1,0:T(8,128)}, u32[]{:S(2)}) copy-start(f32[14,1024]{1,0:T(8,128)} %param.20) | copy-start | bytes 172036
  41.7 3.9 %copy-start.4 = (f32[16,1024]{1,0:T(8,128)S(1)}, f32[16,1024]{1,0:T(8,128)}, u32[]{:S(2)}) copy-start(f32[16,1024]{1,0:T(8,128)} %param.19) | copy-start | bytes 196612
  42.4 49.2 %all-to-all-start = ((bf16[32,3,64,128]{3,2,1,0:T(8,128)(2,1)}), bf16[32,3,64,128]{3,2,1,0:T(8,128)(2,1)S(1)}, u32[]{:S(2)}, u32[]{:S(2)}) async-start(bf16[32,3,64,128]{3,2,1,0:T(8,128)(2,1)} %get-tuple-element.8), calls=%async_computation | async-start | bytes 3145728 | tf_op jit(solution)/shard_map/all_to_all | solution.py:189
  91.6 1.1 copy-start
  92.7 39.1 %copy-start.1 = (bf16[32,3,64,128]{3,2,1,0:T(8,128)(2,1)S(1)}, bf16[32,3,64,128]{3,2,1,0:T(8,128)(2,1)}, u32[]{:S(2)}) copy-start(bf16[32,3,64,128]{3,2,1,0:T(8,128)(2,1)} %get-tuple-element.11) | copy-start | bytes 4718596
Sparse Core Ops, SparseCore 0:
  9.8 30.0 all-gather.4
  41.8 35.2 all-gather.2

commit v2 on v1

v2 whole, which is shorter than its diff:
```python
import functools

import jax
import jax.numpy as jnp
from jax import lax
from jax.experimental import pallas as pl
from jax.experimental.pallas import tpu as pltpu
from jax.sharding import PartitionSpec as P

BLOCK = 256


def lane_iota(rows, width):
    return lax.broadcasted_iota(jnp.int32, (rows, width), 1)


def row_iota(rows, width, start):
    return lax.broadcasted_iota(jnp.int32, (rows, width), 0) + start


def pick(hit):
    return jnp.where(hit, 1.0, 0.0).astype(jnp.bfloat16)


def blend(hit_first, hit_second, share):
    first = jnp.where(hit_first, share, 0.0)
    second = jnp.where(hit_second, 1.0 - share, 0.0)
    return (first + second).astype(jnp.bfloat16)


def dot(left, right):
    return lax.dot_general(left, right, (((1,), (0,)), ((), ())), preferred_element_type=jnp.float32)


def column_of(values):
    return jnp.transpose(jnp.broadcast_to(values, (8, values.shape[1])))[:, 0:1]


def radiate_kernel(
    lon_count,
    perm_ref,
    inc_ref,
    cot_ref,
    back_ref,
    back_w,
    scale_ref,
    tab_ref,
    coarse_ref,
    coarse_w,
    tend_in,
    grad_in,
    stacked,
    cot_out,
    cot_in,
    fields_out,
    fields_in,
    grad_out,
    tend_out,
    tabs,
    wide,
    flat,
    adj,
    heat,
    send_sem,
    recv_sem,
    tab_send,
    tab_recv,
):
    var_count, col_count, width = inc_ref.shape
    devices, segment = cot_out.shape[0], cot_out.shape[1]
    row_count = scale_ref.shape[1]
    band_count = tab_ref.shape[0]
    per_block = BLOCK // segment
    blocks = col_count // BLOCK
    lat, lon = lax.axis_index("lat"), lax.axis_index("lon")
    me = lat * lon_count + lon
    parity = lax.rem(lon, 2)
    partner = lon + 1 - 2 * parity
    home = lax.div(me, per_block)

    def table_copy(source, slot, target, sem):
        return pltpu.make_async_remote_copy(
            src_ref=source,
            dst_ref=tabs.at[slot],
            send_sem=sem,
            recv_sem=tab_recv.at[slot],
            device_id=(lat, target),
            device_id_type=pl.DeviceIdType.MESH,
        )

    def copy(kind, source, landing, target, slot):
        return pltpu.make_async_remote_copy(
            src_ref=source,
            dst_ref=landing,
            send_sem=send_sem.at[kind, target],
            recv_sem=recv_sem.at[kind, slot],
            device_id=(lax.div(target, lon_count), lax.rem(target, lon_count)),
            device_id_type=pl.DeviceIdType.MESH,
        )

    def start_block(kind, source, landing, block):
        for k in range(per_block):
            target = block * per_block + k

            @pl.when(target != me)
            def _():
                copy(kind, source.at[target], landing.at[me], target, me).start()

    def wait_all(kind, landing):
        @pl.loop(1, devices)
        def _(k):
            source = lax.rem(me + k, devices)
            copy(kind, landing.at[source], landing.at[source], source, source).wait_recv()

    def wait_sent(kind, source):
        @pl.loop(1, devices)
        def _(k):
            target = lax.rem(me + k, devices)
            copy(kind, source.at[target], source.at[target], target, target).wait_send()

    def turn(step):
        return lax.rem(step + home + 1, blocks)

    def split_rows(ref, block, values):
        for v in range(var_count):
            piece = values[:, v * width : (v + 1) * width]
            ref[pl.ds(block * per_block, per_block), v] = piece.reshape(per_block, segment, width)

    for j in range(1, lon_count // 2):
        target = lax.rem(lon + 2 * j, lon_count)
        table_copy(tab_ref, lon, target, tab_send.at[0, target]).start()
    table_copy(tab_ref, lon, partner, tab_send.at[0, partner]).start()

    stacked[:, pl.ds(0, width)] = cot_ref[...]
    for v in range(var_count):
        stacked[:, pl.ds((v + 1) * width, width)] = inc_ref[v]

    @pl.loop(0, blocks)
    def _(step):
        block = turn(step)
        rows = pl.ds(pl.multiple_of(block * BLOCK, BLOCK), BLOCK)
        table = pick(column_of(perm_ref[:, rows]) == lane_iota(BLOCK, col_count))
        moved = dot(table, stacked[...]).astype(jnp.bfloat16)
        cot_out[pl.ds(block * per_block, per_block)] = moved[:, :width].reshape(per_block, segment, width)
        split_rows(fields_out, block, moved[:, width:])
        start_block(0, cot_out, cot_in, block)

    @pl.loop(0, blocks)
    def _(step):
        start_block(1, fields_out, fields_in, turn(step))

    cot_in[me] = cot_out[me]
    fields_in[me] = fields_out[me]
    tabs[lon] = tab_ref[...]
    for j in range(1, lon_count // 2):
        source = lax.rem(lon + 2 * j, lon_count)
        table_copy(tabs.at[source], source, source, tab_send.at[0, source]).wait_recv()
        table_copy(tabs.at[source], source, partner, tab_send.at[1, source]).start()
    wait_all(0, cot_in)
    for j in range(lon_count // 2):
        source = lax.rem(partner + 2 * j, lon_count)
        table_copy(tabs.at[source], source, source, tab_send.at[0, source]).wait_recv()
    depth = tab_ref.shape[2]
    for b in range(band_count):
        for v in range(var_count):
            part = tabs[:, b, v].reshape(lon_count * depth, width)
            wide[pl.ds(v * lon_count * depth, lon_count * depth), pl.ds(b * width, width)] = part

    @pl.loop(0, row_count // BLOCK)
    def _(step):
        start = pl.multiple_of(step * BLOCK, BLOCK)
        rows = pl.ds(start, BLOCK)
        spot = row_iota(BLOCK, col_count, start)
        table = blend(back_ref[0:1, :] == spot, back_ref[1:2, :] == spot, back_w[...])
        coarse = dot(table, cot_in[...].reshape(col_count, width))
        scale = jnp.transpose(scale_ref[:, rows])
        lifted = jnp.concatenate([(scale[:, b : b + 1] * coarse).astype(jnp.bfloat16) for b in range(band_count)], axis=1)
        out = lax.dot_general(lifted, wide[...], (((1,), (1,)), ((), ())), preferred_element_type=jnp.float32)
        adj[rows, :] = out.astype(jnp.bfloat16)

    @pl.loop(0, blocks)
    def _(step):
        block = turn(step)
        spot = row_iota(BLOCK, row_count, block * BLOCK)
        table = blend(coarse_ref[0:1, :] == spot, coarse_ref[1:2, :] == spot, coarse_w[...])
        split_rows(grad_out, block, dot(table, adj[...]).astype(jnp.bfloat16))
        start_block(2, grad_out, grad_in, block)

    grad_in[me] = grad_out[me]
    wait_all(1, fields_in)
    for v in range(var_count):
        flat[:, pl.ds(v * width, width)] = fields_in[:, v].reshape(col_count, width)

    @pl.loop(0, row_count // BLOCK)
    def _(step):
        rows = pl.ds(pl.multiple_of(step * BLOCK, BLOCK), BLOCK)
        spot = lane_iota(BLOCK, col_count)
        first, second = column_of(coarse_ref[0:1, rows]), column_of(coarse_ref[1:2, rows])
        table = blend(first == spot, second == spot, column_of(coarse_w[:, rows]))
        coarse = dot(table, flat[...]).astype(jnp.bfloat16)
        scale = jnp.transpose(scale_ref[:, rows])
        total = jnp.zeros((BLOCK, width), jnp.float32)
        for b in range(0, band_count, 2):
            pair = dot(coarse, wide[:, b * width : (b + 2) * width])
            total = total + scale[:, b : b + 1] * pair[:, :width] + scale[:, b + 1 : b + 2] * pair[:, width:]
        heat[rows, :] = total.astype(jnp.bfloat16)

    @pl.loop(0, blocks)
    def _(step):
        block = turn(step)
        rows = pl.ds(pl.multiple_of(block * BLOCK, BLOCK), BLOCK)
        spot = lane_iota(BLOCK, row_count)
        first, second = column_of(back_ref[0:1, rows]), column_of(back_ref[1:2, rows])
        table = blend(first == spot, second == spot, column_of(back_w[:, rows]))
        moved = dot(table, heat[...]).astype(jnp.bfloat16)
        tend_out[pl.ds(block * per_block, per_block)] = moved.reshape(per_block, segment, width)
        start_block(3, tend_out, tend_in, block)

    tend_in[me] = tend_out[me]
    for j in range(1, lon_count // 2):
        other = lax.rem(lon + 2 * j, lon_count)
        table_copy(tab_ref, other, other, tab_send.at[0, other]).wait_send()
        table_copy(tab_ref, other, other, tab_send.at[1, other]).wait_send()
    table_copy(tab_ref, partner, partner, tab_send.at[0, partner]).wait_send()
    wait_all(2, grad_in)
    wait_all(3, tend_in)
    wait_sent(0, cot_out)
    wait_sent(1, fields_out)
    wait_sent(2, grad_out)
    wait_sent(3, tend_out)


def restore_kernel(perm_ref, tend_ref, grad_ref, tend_out, grad_out, stacked):
    devices, var_count, segment, width = grad_ref.shape
    col_count = devices * segment
    stacked[:, pl.ds(0, width)] = tend_ref[...].reshape(col_count, width)
    for v in range(var_count):
        stacked[:, pl.ds((v + 1) * width, width)] = grad_ref[:, v].reshape(col_count, width)

    @pl.loop(0, col_count // BLOCK)
    def one(step):
        rows = pl.ds(pl.multiple_of(step * BLOCK, BLOCK), BLOCK)
        table = pick(perm_ref[...] == row_iota(BLOCK, col_count, step * BLOCK))
        moved = dot(table, stacked[...]).astype(jnp.bfloat16)
        tend_out[rows, :] = moved[:, :width]
        for v in range(var_count):
            grad_out[v, rows, :] = moved[:, (v + 1) * width : (v + 2) * width]


def run(kernel, outs, scratch, flops, args, sems=(), talks=False):
    shapes = [jax.ShapeDtypeStruct(shape, jnp.bfloat16) for shape in outs]
    vmem = pl.BlockSpec(memory_space=pltpu.VMEM)
    return pl.pallas_call(
        kernel,
        out_shape=shapes,
        in_specs=[vmem] * len(args),
        out_specs=[vmem] * len(outs),
        scratch_shapes=[pltpu.VMEM(shape, jnp.bfloat16) for shape in scratch] + [pltpu.SemaphoreType.DMA(shape) for shape in sems],
        compiler_params=pltpu.CompilerParams(vmem_limit_bytes=56 * 1024 * 1024, has_side_effects=talks),
        cost_estimate=pl.CostEstimate(flops=flops, bytes_accessed=4 << 20, transcendentals=0),
    )(*args)


def local(
    increments,
    cotangent,
    owner_perm,
    coarse_index,
    coarse_weight,
    back_index,
    back_weight,
    lw_scale,
    sw_scale,
    sunlit,
    lw_table,
    sw_table,
    *,
    devices,
    lon_count,
):
    table = jnp.concatenate([lw_table, sw_table])
    col_count, var_count, width = increments.shape
    row_count = coarse_weight.shape[0]
    segment = col_count // devices
    thin, split = (devices, segment, width), (devices, var_count, segment, width)
    flat_width = var_count * width
    bands = table.shape[0]
    planes = jnp.transpose(increments, (1, 0, 2))
    stack = (col_count, (var_count + 1) * width)
    move_cost = 2 * col_count * stack[0] * stack[1]
    pad = jnp.zeros((-bands % 8, row_count), jnp.float32)
    scale = jnp.concatenate([lw_scale, sw_scale * sunlit.astype(jnp.float32)[None, :], pad])
    back_w, coarse_w = back_weight[None, :], coarse_weight[None, :]
    back_tend, back_grad = run(
        functools.partial(radiate_kernel, lon_count),
        [thin, split],
        [
            stack,
            thin,
            thin,
            split,
            split,
            split,
            thin,
            (lon_count,) + table.shape,
            (flat_width, bands * width),
            (col_count, flat_width),
            (row_count, flat_width),
            (row_count, width),
        ],
        6 * row_count * bands * flat_width * width,
        (owner_perm, planes, cotangent, back_index, back_w, scale, table, coarse_index, coarse_w),
        sems=((4, devices), (4, devices), (2, lon_count), (lon_count,)),
        talks=True,
    )
    tendency, gradient = run(
        restore_kernel,
        [(col_count, width), (var_count, col_count, width)],
        [stack],
        move_cost,
        (owner_perm, back_tend, back_grad),
    )
    return (tendency, jnp.transpose(gradient, (1, 0, 2)))


def solution(mesh):
    in_specs = (
        P(("lat", "lon"), None, None),
        P(("lat", "lon"), None),
        P(("lat", "lon"), None),
        P(None, ("lat", "lon")),
        P(("lat", "lon")),
        P(None, ("lat", "lon")),
        P(("lat", "lon")),
        P(None, ("lat", "lon")),
        P(None, ("lat", "lon")),
        P(("lat", "lon")),
        P(None, None, "lon", None),
        P(None, None, "lon", None),
    )
    out_specs = (P(("lat", "lon"), None), P(("lat", "lon"), None, None))
    devices = mesh.shape["lat"] * mesh.shape["lon"]

    def body(*args):
        return local(*args, devices=devices, lon_count=mesh.shape["lon"])

    return jax.shard_map(body, mesh=mesh, in_specs=in_specs, out_specs=out_specs, check_vma=False)
```

time: 189 us -> 127 us (0.67); the launches traced: 189 us -> 124 us
  Pallas kernels: 51.8 us -> 119 us
  blocking collectives: 62.4 us -> 0 us
  waiting for transfers between devices: 47.1 us -> 0 us
  between operations: 14.1 us -> 0.65 us
  starting transfers between devices: 10.4 us -> 0 us
  other arithmetic: 0.74 us -> 4.89 us
  local copies, waits for them, and re-layouts: 2.01 us -> 0.08 us
    pallas_call x4 -> x2, Pallas kernels: 51.8 us -> 119 us  [run(): pl.pallas_call(kernel, out_shape=shapes, in_specs=[vmem] * len(args), out...]
    all_to_all x2 -> x0, blocking collectives: 62.4 us -> none  [the longest x1 41 us: local(): lax.all_to_all(sent_grad, axes, split_axis=0, concat_axis=0, tiled=True)]
    all_gather x2 -> x0, waiting for transfers between devices: 30.9 us -> none  [the longest x1 30.9 us: local(): lw_full = lax.all_gather(lw_table, 'lon', axis=2, tiled=True)]
    all_to_all x2 -> x0, waiting for transfers between devices: 14.9 us -> none  [the longest x1 14.9 us: local(): lax.all_to_all(sent_cot, axes, split_axis=0, concat_axis=0, tiled=True)]
    all_to_all x2 -> x0, starting transfers between devices: 10.3 us -> none  [the longest x1 7.31 us: local(): lax.all_to_all(sent_cot, axes, split_axis=0, concat_axis=0, tiled=True)]
    unnamed x12 -> x0, local copies, waits for them, and re-layouts: 1.94 us -> none
  transfers between devices with their start and end apart: 4 -> 0, of which waited for: 2 -> 0; matrix products, arithmetic and copies ran while one was open for 0% -> 0% of each run, Pallas kernels for 13% -> 0%
where the time goes in v2:
time: 127 us; the launch traced here: 124 us
  Pallas kernels  119 us (94%)
  other arithmetic  4.89 us (4%)
    pallas_call x2, Pallas kernels, run(): pl.pallas_call(kernel, out_shape=shapes, in_specs=[vmem] * len(args), out...  119 us

profile of v2, /device:TPU:0, one launch (start us, length us, event | category | flops | bytes accessed | tf_op | source)
XLA Modules:
  0.0 124.3 jit_solution(17927033487443246407)
XLA Ops:
  0.6 0.1 pad.4.clone
  0.7 0.7 convert_element_type.3
  1.4 0.8 broadcast_multiply_fusion
  2.2 1.6 %maximum_maximum_fusion.scale_ref = f32[32,1024]{1,0:T(8,128)} fusion(f32[14,1024]{1,0:T(8,128)S(1)} %broadcast_multiply_fusion, f32[16,1024]{1,0:T(8,128)} %param.19, f32[32]{0:T(128)S(1)} %pad.4.clone), kind=kLoop, calls=%fused_computation.1 | loop fusion | flops 65536 | bytes 254080 | tf_op jit(solution)/shard_map/concatenate | solution.py:292
  3.8 1.8 %pad_maximum_fusion.tab_ref = bf16[30,3,16,128]{3,2,1,0:T(8,128)(2,1)} fusion(bf16[14,3,16,128]{3,2,1,0:T(8,128)(2,1)} %param.23, bf16[16,3,16,128]{3,2,1,0:T(8,128)(2,1)} %param.22), kind=kLoop, calls=%fused_computation | loop fusion | flops 184320 | bytes 737280 | tf_op jit(solution)/shard_map/concatenate | solution.py:281
  5.6 109.7 %shard_map.131 = (bf16[32,64,128]{2,1,0:T(8,128)(2,1)}, bf16[32,3,64,128]{3,2,1,0:T(8,128)(2,1)}) custom-call(s32[1,2048]{1,0:T(1,128)} %perm_ref.3, bf16[3,2048,128]{2,1,0:T(8,128)(2,1)} %bitcast.4, bf16[2048,128]{1,0:T(8,128)(2,1)} %cot_ref.1, s32[2,2048]{1,0:T(2,128)} %back_ref.1, f32[1,2048]{1,0:T(1,128)} %bitcast.5, ...), custom_call_target="tpu_custom_call" | custom-call | flops 9059696640 | bytes 4194304 | tf_op jit(solution)/shard_map/pallas_call | solution.py:253
  115.3 8.9 %shard_map.132 = (bf16[2048,128]{1,0:T(8,128)(2,1)}, bf16[3,2048,128]{2,1,0:T(8,128)(2,1)}) custom-call(s32[1,2048]{1,0:T(1,128)} %perm_ref.3, bf16[32,64,128]{2,1,0:T(8,128)(2,1)} %get-tuple-element.6.tend_ref, bf16[32,3,64,128]{3,2,1,0:T(8,128)(2,1)} %get-tuple-element.7.grad_ref), custom_call_target="tpu_custom_call" | custom-call | flops 4294967296 | bytes 4194304 | tf_op jit(solution)/shard_map/pallas_call | solution.py:253
  (1 shorter events, 0.0 us)

commit v3 on v2

--- a/solution.py
+++ b/solution.py
@@ -43,12 +43,18 @@
     cot_ref,
     back_ref,
     back_w,
-    scale_ref,
-    tab_ref,
+    lw_scale,
+    sw_scale,
+    sun_ref,
+    lw_ref,
+    sw_ref,
     coarse_ref,
     coarse_w,
+    tend_done,
+    grad_done,
     tend_in,
     grad_in,
+    back,
     stacked,
     cot_out,
     cot_in,
@@ -68,8 +74,9 @@
 ):
     var_count, col_count, width = inc_ref.shape
     devices, segment = cot_out.shape[0], cot_out.shape[1]
-    row_count = scale_ref.shape[1]
-    band_count = tab_ref.shape[0]
+    row_count = lw_scale.shape[1]
+    lw_count = lw_ref.shape[0]
+    band_count = lw_count + sw_ref.shape[0]
     per_block = BLOCK // segment
     blocks = col_count // BLOCK
     lat, lon = lax.axis_index("lat"), lax.axis_index("lon")
@@ -118,6 +125,14 @@
             target = lax.rem(me + k, devices)
             copy(kind, source.at[target], source.at[target], target, target).wait_send()
 
+    def scale_of(rows):
+        lit = sun_ref[:, rows].astype(jnp.float32)
+        longwave, shortwave = jnp.transpose(lw_scale[:, rows]), jnp.transpose(sw_scale[:, rows] * lit)
+        return [
+            longwave[:, b : b + 1] if b < lw_count else shortwave[:, b - lw_count : b - lw_count + 1]
+            for b in range(band_count)
+        ]
+
     def turn(step):
         return lax.rem(step + home + 1, blocks)
 
@@ -126,14 +141,16 @@
             piece = values[:, v * width : (v + 1) * width]
             ref[pl.ds(block * per_block, per_block), v] = piece.reshape(per_block, segment, width)
 
-    for j in range(1, lon_count // 2):
-        target = lax.rem(lon + 2 * j, lon_count)
-        table_copy(tab_ref, lon, target, tab_send.at[0, target]).start()
-    table_copy(tab_ref, lon, partner, tab_send.at[0, partner]).start()
-
+    tabs[lon, pl.ds(0, lw_count)] = lw_ref[...]
+    tabs[lon, pl.ds(lw_count, band_count - lw_count)] = sw_ref[...]
     stacked[:, pl.ds(0, width)] = cot_ref[...]
     for v in range(var_count):
         stacked[:, pl.ds((v + 1) * width, width)] = inc_ref[v]
+
+    for j in range(1, lon_count // 2):
+        target = lax.rem(lon + 2 * j, lon_count)
+        table_copy(tabs.at[lon], lon, target, tab_send.at[0, target]).start()
+    table_copy(tabs.at[lon], lon, partner, tab_send.at[0, partner]).start()
 
     @pl.loop(0, blocks)
     def _(step):
@@ -151,7 +168,6 @@
 
     cot_in[me] = cot_out[me]
     fields_in[me] = fields_out[me]
-    tabs[lon] = tab_ref[...]
     for j in range(1, lon_count // 2):
         source = lax.rem(lon + 2 * j, lon_count)
         table_copy(tabs.at[source], source, source, tab_send.at[0, source]).wait_recv()
@@ -160,7 +176,7 @@
     for j in range(lon_count // 2):
         source = lax.rem(partner + 2 * j, lon_count)
         table_copy(tabs.at[source], source, source, tab_send.at[0, source]).wait_recv()
-    depth = tab_ref.shape[2]
+    depth = lw_ref.shape[2]
     for b in range(band_count):
         for v in range(var_count):
             part = tabs[:, b, v].reshape(lon_count * depth, width)
@@ -173,8 +189,8 @@
         spot = row_iota(BLOCK, col_count, start)
         table = blend(back_ref[0:1, :] == spot, back_ref[1:2, :] == spot, back_w[...])
         coarse = dot(table, cot_in[...].reshape(col_count, width))
-        scale = jnp.transpose(scale_ref[:, rows])
-        lifted = jnp.concatenate([(scale[:, b : b + 1] * coarse).astype(jnp.bfloat16) for b in range(band_count)], axis=1)
+        scale = scale_of(rows)
+        lifted = jnp.concatenate([(scale[b] * coarse).astype(jnp.bfloat16) for b in range(band_count)], axis=1)
         out = lax.dot_general(lifted, wide[...], (((1,), (1,)), ((), ())), preferred_element_type=jnp.float32)
         adj[rows, :] = out.astype(jnp.bfloat16)
 
@@ -187,6 +203,12 @@
         start_block(2, grad_out, grad_in, block)
 
     grad_in[me] = grad_out[me]
+
+    @pl.loop(0, blocks)
+    def _(step):
+        start = pl.multiple_of(step * BLOCK, BLOCK)
+        back[pl.ds(start, BLOCK), :] = pick(perm_ref[...] == row_iota(BLOCK, col_count, start))
+
     wait_all(1, fields_in)
     for v in range(var_count):
         flat[:, pl.ds(v * width, width)] = fields_in[:, v].reshape(col_count, width)
@@ -198,11 +220,11 @@
         first, second = column_of(coarse_ref[0:1, rows]), column_of(coarse_ref[1:2, rows])
         table = blend(first == spot, second == spot, column_of(coarse_w[:, rows]))
         coarse = dot(table, flat[...]).astype(jnp.bfloat16)
-        scale = jnp.transpose(scale_ref[:, rows])
+        scale = scale_of(rows)
         total = jnp.zeros((BLOCK, width), jnp.float32)
         for b in range(0, band_count, 2):
             pair = dot(coarse, wide[:, b * width : (b + 2) * width])
-            total = total + scale[:, b : b + 1] * pair[:, :width] + scale[:, b + 1 : b + 2] * pair[:, width:]
+            total = total + scale[b] * pair[:, :width] + scale[b + 1] * pair[:, width:]
         heat[rows, :] = total.astype(jnp.bfloat16)
 
     @pl.loop(0, blocks)
@@ -219,32 +241,31 @@
     tend_in[me] = tend_out[me]
     for j in range(1, lon_count // 2):
         other = lax.rem(lon + 2 * j, lon_count)
-        table_copy(tab_ref, other, other, tab_send.at[0, other]).wait_send()
-        table_copy(tab_ref, other, other, tab_send.at[1, other]).wait_send()
-    table_copy(tab_ref, partner, partner, tab_send.at[0, partner]).wait_send()
+        table_copy(tabs.at[lon], other, other, tab_send.at[0, other]).wait_send()
+        table_copy(tabs.at[lon], other, other, tab_send.at[1, other]).wait_send()
+    table_copy(tabs.at[lon], partner, partner, tab_send.at[0, partner]).wait_send()
     wait_all(2, grad_in)
+    for v in range(var_count):
+        flat[:, pl.ds(v * width, width)] = grad_in[:, v].reshape(col_count, width)
+
+    @pl.loop(0, blocks)
+    def _(step):
+        rows = pl.ds(pl.multiple_of(step * BLOCK, BLOCK), BLOCK)
+        moved = dot(back[rows, :], flat[...]).astype(jnp.bfloat16)
+        for v in range(var_count):
+            grad_done[v, rows, :] = moved[:, v * width : (v + 1) * width]
+
     wait_all(3, tend_in)
+
+    @pl.loop(0, blocks)
+    def _(step):
+        rows = pl.ds(pl.multiple_of(step * BLOCK, BLOCK), BLOCK)
+        tend_done[rows, :] = dot(back[rows, :], tend_in[...].reshape(col_count, width)).astype(jnp.bfloat16)
+
     wait_sent(0, cot_out)
     wait_sent(1, fields_out)
     wait_sent(2, grad_out)
     wait_sent(3, tend_out)
-
-
-def restore_kernel(perm_ref, tend_ref, grad_ref, tend_out, grad_out, stacked):
-    devices, var_count, segment, width = grad_ref.shape
-    col_count = devices * segment
-    stacked[:, pl.ds(0, width)] = tend_ref[...].reshape(col_count, width)
-    for v in range(var_count):
-        stacked[:, pl.ds((v + 1) * width, width)] = grad_ref[:, v].reshape(col_count, width)
-
-    @pl.loop(0, col_count // BLOCK)
-    def one(step):
-        rows = pl.ds(pl.multiple_of(step * BLOCK, BLOCK), BLOCK)
-        table = pick(perm_ref[...] == row_iota(BLOCK, col_count, step * BLOCK))
-        moved = dot(table, stacked[...]).astype(jnp.bfloat16)
-        tend_out[rows, :] = moved[:, :width]
-        for v in range(var_count):
-            grad_out[v, rows, :] = moved[:, (v + 1) * width : (v + 2) * width]
 
 
 def run(kernel, outs, scratch, flops, args, sems=(), talks=False):
@@ -278,23 +299,22 @@
     devices,
     lon_count,
 ):
-    table = jnp.concatenate([lw_table, sw_table])
     col_count, var_count, width = increments.shape
     row_count = coarse_weight.shape[0]
     segment = col_count // devices
     thin, split = (devices, segment, width), (devices, var_count, segment, width)
     flat_width = var_count * width
-    bands = table.shape[0]
+    bands = lw_table.shape[0] + sw_table.shape[0]
     planes = jnp.transpose(increments, (1, 0, 2))
     stack = (col_count, (var_count + 1) * width)
-    move_cost = 2 * col_count * stack[0] * stack[1]
-    pad = jnp.zeros((-bands % 8, row_count), jnp.float32)
-    scale = jnp.concatenate([lw_scale, sw_scale * sunlit.astype(jnp.float32)[None, :], pad])
     back_w, coarse_w = back_weight[None, :], coarse_weight[None, :]
-    back_tend, back_grad = run(
+    tendency, gradient = run(
         functools.partial(radiate_kernel, lon_count),
-        [thin, split],
+        [(col_count, width), (var_count, col_count, width)],
         [
+            thin,
+            split,
+            (col_count, col_count),
             stack,
             thin,
             thin,
@@ -302,23 +322,29 @@
             split,
             split,
             thin,
-            (lon_count,) + table.shape,
+            (lon_count, bands) + lw_table.shape[1:],
             (flat_width, bands * width),
             (col_count, flat_width),
             (row_count, flat_width),
             (row_count, width),
         ],
         6 * row_count * bands * flat_width * width,
-        (owner_perm, planes, cotangent, back_index, back_w, scale, table, coarse_index, coarse_w),
+        (
+            owner_perm,
+            planes,
+            cotangent,
+            back_index,
+            back_w,
+            lw_scale,
+            sw_scale,
+            sunlit[None, :],
+            lw_table,
+            sw_table,
+            coarse_index,
+            coarse_w,
+        ),
         sems=((4, devices), (4, devices), (2, lon_count), (lon_count,)),
         talks=True,
-    )
-    tendency, gradient = run(
-        restore_kernel,
-        [(col_count, width), (var_count, col_count, width)],
-        [stack],
-        move_cost,
-        (owner_perm, back_tend, back_grad),
     )
     return (tendency, jnp.transpose(gradient, (1, 0, 2)))
 

time: 127 us -> 121 us (0.953)
  the two profiles are of different devices: /device:TPU:0 before, /device:TPU:15 now
where the time goes in v3:
time: 121 us
  Pallas kernels  116 us (96%)
  local copies, waits for them, and re-layouts  4.52 us (4%)
    pallas_call x1, Pallas kernels, run(): pl.pallas_call(kernel, out_shape=shapes, in_specs=[vmem] * len(args), out...  116 us
    unnamed x2, local copies, waits for them, and re-layouts  4.52 us

profile of v3, /device:TPU:15, one launch (start us, length us, event | category | flops | bytes accessed | tf_op | source)
XLA Modules:
  0.0 121.0 jit_solution(16821641136035746337)
XLA Ops:
  0.6 115.8 %shard_map.131 = (bf16[2048,128]{1,0:T(8,128)(2,1)}, bf16[3,2048,128]{2,1,0:T(8,128)(2,1)}) custom-call(s32[1,2048]{1,0:T(1,128)} %perm_ref.1, bf16[3,2048,128]{2,1,0:T(8,128)(2,1)} %bitcast.6, bf16[2048,128]{1,0:T(8,128)(2,1)} %cot_ref.1, s32[2,2048]{1,0:T(2,128)} %back_ref.1, f32[1,2048]{1,0:T(1,128)} %bitcast.7, f32[16,1024]{1,0:T(8,128)} %lw_scale.1, ...), custom_call_target="tpu_custom_call" | custom-call | flops 9059696640 | bytes 4194304 | tf_op jit(solution)/shard_map/pallas_call | solution.py:274
  116.5 1.9 %copy.16 = bf16[2048,128]{1,0:T(8,128)(2,1)} copy(bf16[2048,128]{1,0:T(8,128)(2,1)} %get-tuple-element.8) | data formatting | bytes 1048576
  118.4 2.7 %copy.17 = bf16[2048,3,128]{2,0,1:T(8,128)(2,1)} copy(bf16[2048,3,128]{2,0,1:T(8,128)(2,1)} %bitcast.5) | data formatting | bytes 3145728
